TPU v7x, 32 devices: a whole 2x2x4 slice. The times are simulated.
32 devices in a mesh: gx: 4 (over y, core), gy: 4 (over z), gz: 2 (over x).
Axes of the slice: x: 2, y: 2, z: 4, core: 2. Of those that a mesh axis runs over, the one named last changes fastest.
Arguments:
- rhs: float32 [4, 32, 32, 256], P(None, 'gx', 'gy', 'gz'), may hold values from -170 to 170
- basis: bfloat16 [4, 8, 32, 32, 256], P(None, None, 'gx', 'gy', 'gz'), may hold values from -6 to 6
- inertia: float32 [32, 32, 256], P('gx', 'gy', 'gz'), may hold values from 0.5 to 2
- helm: float32 [4], replicated, may hold values from 0.2 to 1
- stiffness: float32 [8, 8], replicated, may hold values from -0.05 to 0.6, as said below
Outputs:
- solution: float32 [4, 32, 32, 256], P(None, 'gx', 'gy', 'gz')
- new_basis: bfloat16 [4, 32, 32, 256], P(None, 'gx', 'gy', 'gz')
Inputs may be any that keep to these rules, and one draw needn't show every extreme that they name: `stiffness`: symmetric; every diagonal entry exceeds the sum of the magnitudes of the other entries of its row.
All inputs are finite; a program needn't handle non-finite values.
Results may differ from a plain program's by a relative error of at most 0.001.
Values sent between devices are 32-bit elements; how exact they have to be, the bound alone decides.
A program may use at most 64 MiB of HBM per device.

v0:
```python
import jax
import jax.numpy as jnp
from jax import lax
from jax.sharding import PartitionSpec as P

ITERS = 2
penalty = 0.15
epsilon = 1e-06
highest = lax.Precision.HIGHEST


def padded_2(block, sides, width):
    for axis, dim in sides:
        count = lax.axis_size(axis)
        forward = [(i, i + 1) for i in range(count - 1)]
        backward = [(target, source) for source, target in forward]
        low = lax.ppermute(
            lax.slice_in_dim(block, block.shape[dim] - width, None, axis=dim), axis, forward
        )
        high = lax.ppermute(lax.slice_in_dim(block, 0, width, axis=dim), axis, backward)
        block = jnp.concatenate([low, block, high], axis=dim)
    return block


def block_matrix(stiffness, size_c):
    points = stiffness.shape[0]
    cells = lax.broadcasted_iota(jnp.int32, (size_c, points), 0)
    slots = lax.broadcasted_iota(jnp.int32, (size_c, points), 1)
    selector = jnp.where(cells % points == slots, 1.0, 0.0).astype(jnp.float32)
    spread_out = jnp.dot(
        jnp.dot(selector, stiffness, precision=highest), selector.T, precision=highest
    )
    rows_block = lax.broadcasted_iota(jnp.int32, (size_c, size_c), 0) // points
    cols_block = lax.broadcasted_iota(jnp.int32, (size_c, size_c), 1) // points
    return jnp.where(rows_block == cols_block, spread_out, 0.0)


def stiffen(vector, stiffness, full_block):
    leading, size_a, size_b, size_c = vector.shape
    points = stiffness.shape[0]
    along_a = jnp.einsum(
        "ij,sajbc->saibc",
        stiffness,
        vector.reshape(leading, size_a // points, points, size_b, size_c),
        precision=highest,
    ).reshape(vector.shape)
    along_b = jnp.einsum(
        "ij,sabjc->sabic",
        stiffness,
        vector.reshape(leading, size_a, size_b // points, points, size_c),
        precision=highest,
    ).reshape(vector.shape)
    along_c = jnp.einsum("sabj,ij->sabi", vector, full_block, precision=highest)
    return along_a + along_b + along_c


def face_terms(vector, padded, points):
    accumulated = jnp.zeros_like(vector)
    neighbours = (
        (1, padded[:, 2:, 1:-1, 1:-1], padded[:, :-2, 1:-1, 1:-1]),
        (2, padded[:, 1:-1, 2:, 1:-1], padded[:, 1:-1, :-2, 1:-1]),
        (3, padded[:, 1:-1, 1:-1, 2:], padded[:, 1:-1, 1:-1, :-2]),
    )
    for axis_pos, higher, lower_side in neighbours:
        position = lax.broadcasted_iota(jnp.int32, vector.shape, axis_pos) % points
        accumulated = accumulated + jnp.where(position == points - 1, vector - higher, 0.0)
        accumulated = accumulated + jnp.where(position == 0, vector - lower_side, 0.0)
    return accumulated


def operate(vector, padded, diagonal, stiffness, full_block):
    return (
        diagonal * vector
        + stiffen(vector, stiffness, full_block)
        + penalty * face_terms(vector, padded, stiffness.shape[0])
    )


def per_solve(values):
    return values[:, None, None, None]


def on_device(rhs, basis, inertia, helm, stiffness):
    point_count = float(
        rhs[0].size * lax.axis_size("gx") * lax.axis_size("gy") * lax.axis_size("gz")
    )
    diagonal = helm[:, None, None, None] * inertia[None]
    full_block = block_matrix(stiffness, rhs.shape[3])

    def apply_all(vector):
        padded = padded_2(vector, (("gx", 1), ("gy", 2), ("gz", 3)), 1)
        return operate(vector, padded, diagonal, stiffness, full_block)

    def project(fields):
        return jnp.einsum("skxyz,sxyz->sk", basis, fields, precision=highest)

    def combine(weights):
        return jnp.einsum("sk,skxyz->sxyz", weights, basis, precision=highest)

    local_coef = project(rhs)
    local_gram = jnp.einsum("skxyz,slxyz->skl", basis, basis, preferred_element_type=jnp.float32)
    coef_sum, gram_sum = lax.psum((local_coef, local_gram), ("gx", "gy", "gz"))
    gram_matrix = gram_sum / point_count
    iterate = combine(coef_sum / point_count)
    residual = rhs - apply_all(iterate)
    direction = jnp.zeros_like(rhs)
    image_dir = jnp.zeros_like(rhs)
    norm_old = None
    step_old = None
    final_moment = None
    final_square = None
    for iteration in range(ITERS):
        image_vec = apply_all(residual)
        norm_part = jnp.sum(residual * residual, axis=(1, 2, 3))
        curv_part = jnp.sum(residual * image_vec, axis=(1, 2, 3))
        if iteration < ITERS - 1:
            norm_now, curvature = lax.psum((norm_part, curv_part), ("gx", "gy", "gz"))
        else:
            norm_now, curvature = lax.psum((norm_part, curv_part), ("gx", "gy", "gz"))
        if iteration == 0:
            conjugacy = jnp.zeros_like(norm_now)
            step_size = norm_now / curvature
        else:
            conjugacy = norm_now / norm_old
            step_size = norm_now / (curvature - conjugacy * norm_now / step_old)
        direction = residual + per_solve(conjugacy) * direction
        image_dir = image_vec + per_solve(conjugacy) * image_dir
        iterate = iterate + per_solve(step_size) * direction
        if iteration < ITERS - 1:
            residual = residual - per_solve(step_size) * image_dir
        norm_old = norm_now
        step_old = step_size
    final_moment, final_square = lax.psum(
        (project(iterate), jnp.sum(iterate * iterate, axis=(1, 2, 3))), ("gx", "gy", "gz")
    )
    weights = final_moment / point_count
    square = final_square / point_count
    spread = (
        square
        - 2.0 * jnp.sum(weights * weights, axis=1)
        + jnp.einsum("sk,skl,sl->s", weights, gram_matrix, weights, precision=highest)
    )
    remainder = iterate - combine(weights)
    new_basis = (remainder * per_solve(lax.rsqrt(spread + epsilon))).astype(jnp.bfloat16)
    return (iterate, new_basis)


def solution(mesh):
    placed = (
        P(None, "gx", "gy", "gz"),
        P(None, None, "gx", "gy", "gz"),
        P("gx", "gy", "gz"),
        P(),
        P(),
    )
    return jax.shard_map(
        on_device,
        mesh=mesh,
        in_specs=placed,
        out_specs=(P(None, "gx", "gy", "gz"), P(None, "gx", "gy", "gz")),
        check_vma=False,
    )
```

profile of v0, /device:TPU:0, one launch (start us, length us, event | category | flops | bytes accessed | tf_op | source)
XLA Modules:
  0.0 254.5 jit_solution(11118584132166019880)
XLA Ops:
  0.7 2.6 %fusion.20 = f32[4,1,8,1,1]{2,1,4,3,0:T(1,128)S(1)} fusion(f32[4,8,8,128,1]{3,4,2,1,0:T(1,128)} %bitcast.131, bf16[4,8,8,8,128]{4,3,2,1,0:T(8,128)(2,1)} %param.6), kind=kOutput, calls=%fused_computation.31 | convolution fusion | flops 3145728 | bytes 655488 | tf_op jit(solution)/shard_map/skxyz,sxyz->sk/dot_general | solution.py:95
  3.3 41.9 %psum.56 = f32[4,8]{1,0:T(4,128)S(1)} all-reduce(f32[4,8]{1,0:T(4,128)S(1)} %bitcast.130), channel_id=1, replica_groups=mesh['gx'=4,'gy'=4,'gz'=2] {'gx','gy','gz'}, use_global_device_ids=true, to_apply=%region_0.1 | all-reduce | flops 32 | bytes 256 | tf_op jit(solution)/shard_map/psum | solution.py:102
  46.0 1.3 collective-permute-start
  47.3 3.0 %collective-permute-start.1 = (f32[4,1,8,128]{3,1,2,0:T(1,128)S(1)}, f32[4,1,8,128]{3,1,2,0:T(1,128)S(1)}, u32[]{:S(2)}, u32[]{:S(2)}) collective-permute-start(f32[4,1,8,128]{3,1,2,0:T(1,128)S(1)} %get-tuple-element.39), channel_id=1, source_target_pairs={{0,8},{8,16},{16,24},{1,9},{9,17},{17,25},{2,10},{10,18},{18,26},{... | collective-permute-start | bytes 49160 | tf_op jit(solution)/shard_map/ppermute | solution.py:17
  51.6 1.3 collective-permute-start.2
  52.9 4.5 %collective-permute-start.3 = (f32[4,10,1,128]{3,1,2,0:T(8,128)S(1)}, f32[4,10,1,128]{3,1,2,0:T(8,128)S(1)}, u32[]{:S(2)}, u32[]{:S(2)}) collective-permute-start(f32[4,10,1,128]{3,1,2,0:T(8,128)S(1)} %get-tuple-element.33), channel_id=1, source_target_pairs={{0,2},{2,4},{4,6},{1,3},{3,5},{5,7},{8,10},{10,12},{12,14},{9,11},... | collective-permute-start | bytes 61448 | tf_op jit(solution)/shard_map/ppermute | solution.py:17
  57.5 1.6 collective-permute-done.3
  60.6 4.6 %collective-permute-start.5 = (f32[4,10,10,1]{3,1,2,0:T(8,128)S(1)}, f32[4,10,10,1]{3,1,2,0:T(8,128)S(1)}, u32[]{:S(2)}, u32[]{:S(2)}) collective-permute-start(f32[4,10,10,1]{3,1,2,0:T(8,128)S(1)} %get-tuple-element.28), channel_id=1, source_target_pairs={{0,1},{2,3},{4,5},{6,7},{8,9},{10,11},{12,13},{14,15},{16,17},{18,... | collective-permute-start | bytes 4808 | tf_op jit(solution)/shard_map/ppermute | solution.py:17
  65.2 6.3 %collective-permute-done.4 = f32[4,10,10,1]{3,1,2,0:T(8,128)S(1)} collective-permute-done((f32[4,10,10,1]{3,1,2,0:T(8,128)S(1)}, f32[4,10,10,1]{3,1,2,0:T(8,128)S(1)}, u32[]{:S(2)}, u32[]{:S(2)}) %collective-permute-start.4) | collective-permute-done | bytes 1632 | tf_op jit(solution)/shard_map/ppermute | solution.py:20
  75.1 3.0 %collective-permute-start.7 = (f32[4,1,8,128]{3,1,2,0:T(1,128)S(1)}, f32[4,1,8,128]{3,1,2,0:T(1,128)S(1)}, u32[]{:S(2)}, u32[]{:S(2)}) collective-permute-start(f32[4,1,8,128]{3,1,2,0:T(1,128)S(1)} %get-tuple-element.37), channel_id=1, source_target_pairs={{0,8},{8,16},{16,24},{1,9},{9,17},{17,25},{2,10},{10,18},{18,26},{... | collective-permute-start | bytes 49160 | tf_op jit(solution)/shard_map/ppermute | solution.py:17
  80.3 4.6 %collective-permute-start.9 = (f32[4,10,1,128]{3,1,2,0:T(8,128)S(1)}, f32[4,10,1,128]{3,1,2,0:T(8,128)S(1)}, u32[]{:S(2)}, u32[]{:S(2)}) collective-permute-start(f32[4,10,1,128]{3,1,2,0:T(8,128)S(1)} %get-tuple-element.31), channel_id=1, source_target_pairs={{0,2},{2,4},{4,6},{1,3},{3,5},{5,7},{8,10},{10,12},{12,14},{9,11},... | collective-permute-start | bytes 61448 | tf_op jit(solution)/shard_map/ppermute | solution.py:17
  85.1 1.3 collective-permute-done.9
  88.0 4.6 %collective-permute-start.11 = (f32[4,10,10,1]{3,1,2,0:T(8,128)S(1)}, f32[4,10,10,1]{3,1,2,0:T(8,128)S(1)}, u32[]{:S(2)}, u32[]{:S(2)}) collective-permute-start(f32[4,10,10,1]{3,1,2,0:T(8,128)S(1)} %get-tuple-element.26), channel_id=1, source_target_pairs={{0,1},{2,3},{4,5},{6,7},{8,9},{10,11},{12,13},{14,15},{16,17},{18,... | collective-permute-start | bytes 4808 | tf_op jit(solution)/shard_map/ppermute | solution.py:17
  92.8 5.2 %collective-permute-done.10 = f32[4,10,10,1]{3,1,2,0:T(8,128)S(1)} collective-permute-done((f32[4,10,10,1]{3,1,2,0:T(8,128)S(1)}, f32[4,10,10,1]{3,1,2,0:T(8,128)S(1)}, u32[]{:S(2)}, u32[]{:S(2)}) %collective-permute-start.10) | collective-permute-done | bytes 1632 | tf_op jit(solution)/shard_map/ppermute | solution.py:20
  99.7 41.8 %all-reduce.2 = (f32[4]{0:T(128)S(1)}, f32[4]{0:T(128)S(1)}) all-reduce(f32[4]{0:T(128)S(1)} %get-tuple-element.7, f32[4]{0:T(128)S(1)} %get-tuple-element.6), channel_id=1, replica_groups=mesh['gx'=4,'gy'=4,'gz'=2] {'gx','gy','gz'}, use_global_device_ids=true, to_apply=%region_2.3 | all-reduce | flops 8 | bytes 64 | tf_op jit(solution)/shard_map/psum | solution.py:117
  143.0 3.0 %collective-permute-start.13 = (f32[4,1,8,128]{3,1,2,0:T(1,128)S(1)}, f32[4,1,8,128]{3,1,2,0:T(1,128)S(1)}, u32[]{:S(2)}, u32[]{:S(2)}) collective-permute-start(f32[4,1,8,128]{3,1,2,0:T(1,128)S(1)} %get-tuple-element.35), channel_id=1, source_target_pairs={{0,8},{8,16},{16,24},{1,9},{9,17},{17,25},{2,10},{10,18},{18,26},{... | collective-permute-start | bytes 49160 | tf_op jit(solution)/shard_map/ppermute | solution.py:17
  146.9 1.3 collective-permute-start.14
  148.2 4.5 %collective-permute-start.15 = (f32[4,10,1,128]{3,1,2,0:T(8,128)S(1)}, f32[4,10,1,128]{3,1,2,0:T(8,128)S(1)}, u32[]{:S(2)}, u32[]{:S(2)}) collective-permute-start(f32[4,10,1,128]{3,1,2,0:T(8,128)S(1)} %get-tuple-element.29), channel_id=1, source_target_pairs={{0,2},{2,4},{4,6},{1,3},{3,5},{5,7},{8,10},{10,12},{12,14},{9,11},... | collective-permute-start | bytes 61448 | tf_op jit(solution)/shard_map/ppermute | solution.py:17
  153.0 1.3 collective-permute-done.15
  155.9 4.6 %collective-permute-start.17 = (f32[4,10,10,1]{3,1,2,0:T(8,128)S(1)}, f32[4,10,10,1]{3,1,2,0:T(8,128)S(1)}, u32[]{:S(2)}, u32[]{:S(2)}) collective-permute-start(f32[4,10,10,1]{3,1,2,0:T(8,128)S(1)} %get-tuple-element.24), channel_id=1, source_target_pairs={{0,1},{2,3},{4,5},{6,7},{8,9},{10,11},{12,13},{14,15},{16,17},{18,... | collective-permute-start | bytes 4808 | tf_op jit(solution)/shard_map/ppermute | solution.py:17
  160.7 6.1 %collective-permute-done.16 = f32[4,10,10,1]{3,1,2,0:T(8,128)S(1)} collective-permute-done((f32[4,10,10,1]{3,1,2,0:T(8,128)S(1)}, f32[4,10,10,1]{3,1,2,0:T(8,128)S(1)}, u32[]{:S(2)}, u32[]{:S(2)}) %collective-permute-start.16) | collective-permute-done | bytes 1632 | tf_op jit(solution)/shard_map/ppermute | solution.py:20
  168.5 41.5 %all-reduce.1 = (f32[4]{0:T(128)S(1)}, f32[4]{0:T(128)S(1)}) all-reduce(f32[4]{0:T(128)S(1)} %get-tuple-element.21, f32[4]{0:T(128)S(1)} %fusion.11), channel_id=1, replica_groups=mesh['gx'=4,'gy'=4,'gz'=2] {'gx','gy','gz'}, use_global_device_ids=true, to_apply=%region_6.7 | all-reduce | flops 8 | bytes 64 | tf_op jit(solution)/shard_map/psum | solution.py:119
  211.0 1.6 fusion.16
  212.6 40.1 %all-reduce = (f32[4,8]{1,0:T(4,128)S(1)}, f32[4,8,8]{2,1,0:T(8,128)S(1)}, f32[4]{0:T(128)S(1)}) all-reduce(f32[4,8]{1,0:T(4,128)S(1)} %bitcast.129, f32[4,8,8]{2,1,0:T(8,128)S(1)} %convolution_bitcast_fusion.3, f32[4]{0:T(128)S(1)} %get-tuple-element.17), channel_id=1, replica_groups=mesh['gx'=4,'gy'=4,'gz'=2] {'gx','gy','gz'}, use_global_device_ids=true, to_apply=%region_9.10 | all-reduce | flops 292 | bytes 2336 | tf_op jit(solution)/shard_map/psum | solution.py:133
  (74 shorter events, 21.6 us)
Async XLA Ops:
  0.6 49.8 %copy-start = (f32[8,8]{1,0:T(8,128)S(1)}, f32[8,8]{1,0:T(8,128)}, u32[]{:S(2)}) copy-start(f32[8,8]{1,0:T(8,128)} %param.9) | copy-start | bytes 772
  0.6 44.6 %copy-start.1 = (bf16[4,8,8,8,128]{4,3,2,1,0:T(8,128)(2,1)S(1)}, bf16[4,8,8,8,128]{4,3,2,1,0:T(8,128)(2,1)}, u32[]{:S(2)}) copy-start(bf16[4,8,8,8,128]{4,3,2,1,0:T(8,128)(2,1)} %param.6) | copy-start | bytes 1572868
  46.0 5.6 %collective-permute-start = (f32[4,1,8,128]{3,1,2,0:T(1,128)S(1)}, f32[4,1,8,128]{3,1,2,0:T(1,128)S(1)}, u32[]{:S(2)}, u32[]{:S(2)}) collective-permute-start(f32[4,1,8,128]{3,1,2,0:T(1,128)S(1)} %get-tuple-element.40), channel_id=1, source_target_pairs={{8,0},{16,8},{24,16},{9,1},{17,9},{25,17},{10,2},{18,10},{26,18},{... | collective-permute-start | bytes 49160 | tf_op jit(solution)/shard_map/ppermute | solution.py:20
  47.3 4.3 %collective-permute-start.1 = (f32[4,1,8,128]{3,1,2,0:T(1,128)S(1)}, f32[4,1,8,128]{3,1,2,0:T(1,128)S(1)}, u32[]{:S(2)}, u32[]{:S(2)}) collective-permute-start(f32[4,1,8,128]{3,1,2,0:T(1,128)S(1)} %get-tuple-element.39), channel_id=1, source_target_pairs={{0,8},{8,16},{16,24},{1,9},{9,17},{17,25},{2,10},{10,18},{18,26},{... | collective-permute-start | bytes 49160 | tf_op jit(solution)/shard_map/ppermute | solution.py:17
  51.6 5.9 %collective-permute-start.2 = (f32[4,10,1,128]{3,1,2,0:T(8,128)S(1)}, f32[4,10,1,128]{3,1,2,0:T(8,128)S(1)}, u32[]{:S(2)}, u32[]{:S(2)}) collective-permute-start(f32[4,10,1,128]{3,1,2,0:T(8,128)S(1)} %get-tuple-element.34), channel_id=1, source_target_pairs={{2,0},{4,2},{6,4},{3,1},{5,3},{7,5},{10,8},{12,10},{14,12},{11,9},... | collective-permute-start | bytes 61448 | tf_op jit(solution)/shard_map/ppermute | solution.py:20
  52.9 6.1 %collective-permute-start.3 = (f32[4,10,1,128]{3,1,2,0:T(8,128)S(1)}, f32[4,10,1,128]{3,1,2,0:T(8,128)S(1)}, u32[]{:S(2)}, u32[]{:S(2)}) collective-permute-start(f32[4,10,1,128]{3,1,2,0:T(8,128)S(1)} %get-tuple-element.33), channel_id=1, source_target_pairs={{0,2},{2,4},{4,6},{1,3},{3,5},{5,7},{8,10},{10,12},{12,14},{9,11},... | collective-permute-start | bytes 61448 | tf_op jit(solution)/shard_map/ppermute | solution.py:17
  59.1 6.1 %copy-start.2 = (f32[8,8,128]{2,1,0:T(8,128)S(1)}, f32[8,8,128]{2,1,0:T(8,128)}, u32[]{:S(2)}) copy-start(f32[8,8,128]{2,1,0:T(8,128)} %param.7) | copy-start | bytes 98308
  59.1 13.6 %copy-start.3 = (f32[4,8,8,128]{3,2,1,0:T(8,128)S(1)}, f32[4,8,8,128]{3,2,1,0:T(8,128)}, u32[]{:S(2)}) copy-start(f32[4,8,8,128]{3,2,1,0:T(8,128)} %param.5) | copy-start | bytes 393220
  59.3 12.3 %collective-permute-start.4 = (f32[4,10,10,1]{3,1,2,0:T(8,128)S(1)}, f32[4,10,10,1]{3,1,2,0:T(8,128)S(1)}, u32[]{:S(2)}, u32[]{:S(2)}) collective-permute-start(f32[4,10,10,1]{3,1,2,0:T(8,128)S(1)} %get-tuple-element.27), channel_id=1, source_target_pairs={{1,0},{3,2},{5,4},{7,6},{9,8},{11,10},{13,12},{15,14},{17,16},{19,... | collective-permute-start | bytes 4808 | tf_op jit(solution)/shard_map/ppermute | solution.py:20
  60.6 12.2 %collective-permute-start.5 = (f32[4,10,10,1]{3,1,2,0:T(8,128)S(1)}, f32[4,10,10,1]{3,1,2,0:T(8,128)S(1)}, u32[]{:S(2)}, u32[]{:S(2)}) collective-permute-start(f32[4,10,10,1]{3,1,2,0:T(8,128)S(1)} %get-tuple-element.28), channel_id=1, source_target_pairs={{0,1},{2,3},{4,5},{6,7},{8,9},{10,11},{12,13},{14,15},{16,17},{18,... | collective-permute-start | bytes 4808 | tf_op jit(solution)/shard_map/ppermute | solution.py:17
  72.7 0.7 copy-start.4
  73.8 4.3 %collective-permute-start.6 = (f32[4,1,8,128]{3,1,2,0:T(1,128)S(1)}, f32[4,1,8,128]{3,1,2,0:T(1,128)S(1)}, u32[]{:S(2)}, u32[]{:S(2)}) collective-permute-start(f32[4,1,8,128]{3,1,2,0:T(1,128)S(1)} %get-tuple-element.38), channel_id=1, source_target_pairs={{8,0},{16,8},{24,16},{9,1},{17,9},{25,17},{10,2},{18,10},{26,18},{... | collective-permute-start | bytes 49160 | tf_op jit(solution)/shard_map/ppermute | solution.py:20
  75.1 3.9 %collective-permute-start.7 = (f32[4,1,8,128]{3,1,2,0:T(1,128)S(1)}, f32[4,1,8,128]{3,1,2,0:T(1,128)S(1)}, u32[]{:S(2)}, u32[]{:S(2)}) collective-permute-start(f32[4,1,8,128]{3,1,2,0:T(1,128)S(1)} %get-tuple-element.37), channel_id=1, source_target_pairs={{0,8},{8,16},{16,24},{1,9},{9,17},{17,25},{2,10},{10,18},{18,26},{... | collective-permute-start | bytes 49160 | tf_op jit(solution)/shard_map/ppermute | solution.py:17
  79.0 6.1 %collective-permute-start.8 = (f32[4,10,1,128]{3,1,2,0:T(8,128)S(1)}, f32[4,10,1,128]{3,1,2,0:T(8,128)S(1)}, u32[]{:S(2)}, u32[]{:S(2)}) collective-permute-start(f32[4,10,1,128]{3,1,2,0:T(8,128)S(1)} %get-tuple-element.32), channel_id=1, source_target_pairs={{2,0},{4,2},{6,4},{3,1},{5,3},{7,5},{10,8},{12,10},{14,12},{11,9},... | collective-permute-start | bytes 61448 | tf_op jit(solution)/shard_map/ppermute | solution.py:20
  80.3 6.1 %collective-permute-start.9 = (f32[4,10,1,128]{3,1,2,0:T(8,128)S(1)}, f32[4,10,1,128]{3,1,2,0:T(8,128)S(1)}, u32[]{:S(2)}, u32[]{:S(2)}) collective-permute-start(f32[4,10,1,128]{3,1,2,0:T(8,128)S(1)} %get-tuple-element.31), channel_id=1, source_target_pairs={{0,2},{2,4},{4,6},{1,3},{3,5},{5,7},{8,10},{10,12},{12,14},{9,11},... | collective-permute-start | bytes 61448 | tf_op jit(solution)/shard_map/ppermute | solution.py:17
  86.7 11.4 %collective-permute-start.10 = (f32[4,10,10,1]{3,1,2,0:T(8,128)S(1)}, f32[4,10,10,1]{3,1,2,0:T(8,128)S(1)}, u32[]{:S(2)}, u32[]{:S(2)}) collective-permute-start(f32[4,10,10,1]{3,1,2,0:T(8,128)S(1)} %get-tuple-element.25), channel_id=1, source_target_pairs={{1,0},{3,2},{5,4},{7,6},{9,8},{11,10},{13,12},{15,14},{17,16},{19,... | collective-permute-start | bytes 4808 | tf_op jit(solution)/shard_map/ppermute | solution.py:20
  88.0 11.3 %collective-permute-start.11 = (f32[4,10,10,1]{3,1,2,0:T(8,128)S(1)}, f32[4,10,10,1]{3,1,2,0:T(8,128)S(1)}, u32[]{:S(2)}, u32[]{:S(2)}) collective-permute-start(f32[4,10,10,1]{3,1,2,0:T(8,128)S(1)} %get-tuple-element.26), channel_id=1, source_target_pairs={{0,1},{2,3},{4,5},{6,7},{8,9},{10,11},{12,13},{14,15},{16,17},{18,... | collective-permute-start | bytes 4808 | tf_op jit(solution)/shard_map/ppermute | solution.py:17
  141.7 4.9 %collective-permute-start.12 = (f32[4,1,8,128]{3,1,2,0:T(1,128)S(1)}, f32[4,1,8,128]{3,1,2,0:T(1,128)S(1)}, u32[]{:S(2)}, u32[]{:S(2)}) collective-permute-start(f32[4,1,8,128]{3,1,2,0:T(1,128)S(1)} %get-tuple-element.36), channel_id=1, source_target_pairs={{8,0},{16,8},{24,16},{9,1},{17,9},{25,17},{10,2},{18,10},{26,18},{... | collective-permute-start | bytes 49160 | tf_op jit(solution)/shard_map/ppermute | solution.py:20
  143.0 3.9 %collective-permute-start.13 = (f32[4,1,8,128]{3,1,2,0:T(1,128)S(1)}, f32[4,1,8,128]{3,1,2,0:T(1,128)S(1)}, u32[]{:S(2)}, u32[]{:S(2)}) collective-permute-start(f32[4,1,8,128]{3,1,2,0:T(1,128)S(1)} %get-tuple-element.35), channel_id=1, source_target_pairs={{0,8},{8,16},{16,24},{1,9},{9,17},{17,25},{2,10},{10,18},{18,26},{... | collective-permute-start | bytes 49160 | tf_op jit(solution)/shard_map/ppermute | solution.py:17
  146.9 6.1 %collective-permute-start.14 = (f32[4,10,1,128]{3,1,2,0:T(8,128)S(1)}, f32[4,10,1,128]{3,1,2,0:T(8,128)S(1)}, u32[]{:S(2)}, u32[]{:S(2)}) collective-permute-start(f32[4,10,1,128]{3,1,2,0:T(8,128)S(1)} %get-tuple-element.30), channel_id=1, source_target_pairs={{2,0},{4,2},{6,4},{3,1},{5,3},{7,5},{10,8},{12,10},{14,12},{11,9},... | collective-permute-start | bytes 61448 | tf_op jit(solution)/shard_map/ppermute | solution.py:20
  148.2 6.1 %collective-permute-start.15 = (f32[4,10,1,128]{3,1,2,0:T(8,128)S(1)}, f32[4,10,1,128]{3,1,2,0:T(8,128)S(1)}, u32[]{:S(2)}, u32[]{:S(2)}) collective-permute-start(f32[4,10,1,128]{3,1,2,0:T(8,128)S(1)} %get-tuple-element.29), channel_id=1, source_target_pairs={{0,2},{2,4},{4,6},{1,3},{3,5},{5,7},{8,10},{10,12},{12,14},{9,11},... | collective-permute-start | bytes 61448 | tf_op jit(solution)/shard_map/ppermute | solution.py:17
  154.6 12.3 %collective-permute-start.16 = (f32[4,10,10,1]{3,1,2,0:T(8,128)S(1)}, f32[4,10,10,1]{3,1,2,0:T(8,128)S(1)}, u32[]{:S(2)}, u32[]{:S(2)}) collective-permute-start(f32[4,10,10,1]{3,1,2,0:T(8,128)S(1)} %get-tuple-element.23), channel_id=1, source_target_pairs={{1,0},{3,2},{5,4},{7,6},{9,8},{11,10},{13,12},{15,14},{17,16},{19,... | collective-permute-start | bytes 4808 | tf_op jit(solution)/shard_map/ppermute | solution.py:20
  155.9 12.2 %collective-permute-start.17 = (f32[4,10,10,1]{3,1,2,0:T(8,128)S(1)}, f32[4,10,10,1]{3,1,2,0:T(8,128)S(1)}, u32[]{:S(2)}, u32[]{:S(2)}) collective-permute-start(f32[4,10,10,1]{3,1,2,0:T(8,128)S(1)} %get-tuple-element.24), channel_id=1, source_target_pairs={{0,1},{2,3},{4,5},{6,7},{8,9},{10,11},{12,13},{14,15},{16,17},{18,... | collective-permute-start | bytes 4808 | tf_op jit(solution)/shard_map/ppermute | solution.py:17
where the time goes:
time: 256 us; the launch traced here: 255 us
  blocking collectives  165 us (64%)
  starting transfers between devices  48.1 us (19%)
  waiting for transfers between devices  26.6 us (10%)
  matrix products  9.83 us (4%)
  local copies, waits for them, and re-layouts  2.59 us (1%)
    psum x2, blocking collectives, on_device(): norm_now, curvature = lax.psum((norm_part, curv_part), ('gx', 'gy', 'gz'))  83.3 us
    psum x1, blocking collectives, on_device(): coef_sum, gram_sum = lax.psum((local_coef, local_gram), ('gx', 'gy', 'gz'))  41.9 us
    psum x1, blocking collectives, on_device(): lax.psum((project(iterate), jnp.sum(iterate * iterate, axis=(1, 2, 3))),...  40.1 us
    ppermute x9, starting transfers between devices, padded_2(): lax.ppermute(lax.slice_in_dim(block, block.shape[dim] - width, None, axis...  36.5 us
    ppermute x9, waiting for transfers between devices, padded_2(): lax.ppermute(lax.slice_in_dim(block, 0, width, axis=dim), axis, backward)  17.7 us
    ppermute x9, starting transfers between devices, padded_2(): lax.ppermute(lax.slice_in_dim(block, 0, width, axis=dim), axis, backward)  11.6 us
    ppermute x9, waiting for transfers between devices, padded_2(): lax.ppermute(lax.slice_in_dim(block, block.shape[dim] - width, None, axis...  8.87 us
  transfers between devices with their start and end apart: 18, of which 11 were waited for; matrix products, arithmetic and copies ran while one was open for 1% of the time, Pallas kernels for 0%

commit v1 on v0

--- a/solution.py
+++ b/solution.py
@@ -130,8 +130,11 @@
             residual = residual - per_solve(step_size) * image_dir
         norm_old = norm_now
         step_old = step_size
-    final_moment, final_square = lax.psum(
-        (project(iterate), jnp.sum(iterate * iterate, axis=(1, 2, 3))), ("gx", "gy", "gz")
+    final_moment, final_square = jax.lax.psum(
+        jax.lax.psum(
+            (project(iterate), jnp.sum(iterate * iterate, axis=(1, 2, 3))), axis_name=("gy", "gz")
+        ),
+        axis_name="gx",
     )
     weights = final_moment / point_count
     square = final_square / point_count

time: 256 us -> 242 us (0.945)
  blocking collectives: 165 us -> 152 us
    psum x1 -> x2, blocking collectives: 40.1 us -> 26.8 us  [the longest x1 21.1 us: on_device(): jax.lax.psum((project(iterate), jnp.sum(iterate * iterate, axis=(1, 2, 3)...]
where the time goes in v1:
time: 242 us; the launch traced here: 241 us
  blocking collectives  152 us (63%)
  starting transfers between devices  48.1 us (20%)
  waiting for transfers between devices  26.6 us (11%)
  matrix products  9.83 us (4%)
  local copies, waits for them, and re-layouts  2.59 us (1%)
    psum x2, blocking collectives, on_device(): norm_now, curvature = lax.psum((norm_part, curv_part), ('gx', 'gy', 'gz'))  83.5 us
    psum x1, blocking collectives, on_device(): coef_sum, gram_sum = lax.psum((local_coef, local_gram), ('gx', 'gy', 'gz'))  41.9 us
    ppermute x9, starting transfers between devices, padded_2(): lax.ppermute(lax.slice_in_dim(block, block.shape[dim] - width, None, axis...  36.5 us
    psum x1, blocking collectives, on_device(): jax.lax.psum((project(iterate), jnp.sum(iterate * iterate, axis=(1, 2, 3)...  21.1 us
    ppermute x9, waiting for transfers between devices, padded_2(): lax.ppermute(lax.slice_in_dim(block, 0, width, axis=dim), axis, backward)  17.7 us
    ppermute x9, starting transfers between devices, padded_2(): lax.ppermute(lax.slice_in_dim(block, 0, width, axis=dim), axis, backward)  11.6 us
    ppermute x9, waiting for transfers between devices, padded_2(): lax.ppermute(lax.slice_in_dim(block, block.shape[dim] - width, None, axis...  8.87 us
    psum x1, blocking collectives, on_device(): jax.lax.psum(jax.lax.psum((project(iterate), jnp.sum(iterate * iterate, a...  5.65 us
  transfers between devices with their start and end apart: 18, of which 11 were waited for; matrix products, arithmetic and copies ran while one was open for 1% of the time, Pallas kernels for 0%

profile of v1, /device:TPU:0, one launch (start us, length us, event | category | flops | bytes accessed | tf_op | source)
XLA Modules:
  0.0 241.3 jit_solution(6364068892591150914)
XLA Ops:
  0.7 2.6 %fusion.20 = f32[4,1,8,1,1]{2,1,4,3,0:T(1,128)S(1)} fusion(f32[4,8,8,128,1]{3,4,2,1,0:T(1,128)} %bitcast.131, bf16[4,8,8,8,128]{4,3,2,1,0:T(8,128)(2,1)} %param.6), kind=kOutput, calls=%fused_computation.31 | convolution fusion | flops 3145728 | bytes 655488 | tf_op jit(solution)/shard_map/skxyz,sxyz->sk/dot_general | solution.py:95
  3.3 41.9 %psum.70 = f32[4,8]{1,0:T(4,128)S(1)} all-reduce(f32[4,8]{1,0:T(4,128)S(1)} %bitcast.130), channel_id=1, replica_groups=mesh['gx'=4,'gy'=4,'gz'=2] {'gx','gy','gz'}, use_global_device_ids=true, to_apply=%region_0.1 | all-reduce | flops 32 | bytes 256 | tf_op jit(solution)/shard_map/psum | solution.py:102
  47.3 3.0 %collective-permute-start.1 = (f32[4,1,8,128]{3,1,2,0:T(1,128)S(1)}, f32[4,1,8,128]{3,1,2,0:T(1,128)S(1)}, u32[]{:S(2)}, u32[]{:S(2)}) collective-permute-start(f32[4,1,8,128]{3,1,2,0:T(1,128)S(1)} %get-tuple-element.41), channel_id=1, source_target_pairs={{0,8},{8,16},{16,24},{1,9},{9,17},{17,25},{2,10},{10,18},{18,26},{... | collective-permute-start | bytes 49160 | tf_op jit(solution)/shard_map/ppermute | solution.py:17
  51.6 1.3 collective-permute-start.2
  52.9 4.5 %collective-permute-start.3 = (f32[4,10,1,128]{3,1,2,0:T(8,128)S(1)}, f32[4,10,1,128]{3,1,2,0:T(8,128)S(1)}, u32[]{:S(2)}, u32[]{:S(2)}) collective-permute-start(f32[4,10,1,128]{3,1,2,0:T(8,128)S(1)} %get-tuple-element.35), channel_id=1, source_target_pairs={{0,2},{2,4},{4,6},{1,3},{3,5},{5,7},{8,10},{10,12},{12,14},{9,11},... | collective-permute-start | bytes 61448 | tf_op jit(solution)/shard_map/ppermute | solution.py:17
  57.5 1.6 collective-permute-done.3
  60.6 4.6 %collective-permute-start.5 = (f32[4,10,10,1]{3,1,2,0:T(8,128)S(1)}, f32[4,10,10,1]{3,1,2,0:T(8,128)S(1)}, u32[]{:S(2)}, u32[]{:S(2)}) collective-permute-start(f32[4,10,10,1]{3,1,2,0:T(8,128)S(1)} %get-tuple-element.30), channel_id=1, source_target_pairs={{0,1},{2,3},{4,5},{6,7},{8,9},{10,11},{12,13},{14,15},{16,17},{18,... | collective-permute-start | bytes 4808 | tf_op jit(solution)/shard_map/ppermute | solution.py:17
  65.2 6.3 %collective-permute-done.4 = f32[4,10,10,1]{3,1,2,0:T(8,128)S(1)} collective-permute-done((f32[4,10,10,1]{3,1,2,0:T(8,128)S(1)}, f32[4,10,10,1]{3,1,2,0:T(8,128)S(1)}, u32[]{:S(2)}, u32[]{:S(2)}) %collective-permute-start.4) | collective-permute-done | bytes 1632 | tf_op jit(solution)/shard_map/ppermute | solution.py:20
  75.1 3.0 %collective-permute-start.7 = (f32[4,1,8,128]{3,1,2,0:T(1,128)S(1)}, f32[4,1,8,128]{3,1,2,0:T(1,128)S(1)}, u32[]{:S(2)}, u32[]{:S(2)}) collective-permute-start(f32[4,1,8,128]{3,1,2,0:T(1,128)S(1)} %get-tuple-element.39), channel_id=1, source_target_pairs={{0,8},{8,16},{16,24},{1,9},{9,17},{17,25},{2,10},{10,18},{18,26},{... | collective-permute-start | bytes 49160 | tf_op jit(solution)/shard_map/ppermute | solution.py:17
  80.3 4.6 %collective-permute-start.9 = (f32[4,10,1,128]{3,1,2,0:T(8,128)S(1)}, f32[4,10,1,128]{3,1,2,0:T(8,128)S(1)}, u32[]{:S(2)}, u32[]{:S(2)}) collective-permute-start(f32[4,10,1,128]{3,1,2,0:T(8,128)S(1)} %get-tuple-element.33), channel_id=1, source_target_pairs={{0,2},{2,4},{4,6},{1,3},{3,5},{5,7},{8,10},{10,12},{12,14},{9,11},... | collective-permute-start | bytes 61448 | tf_op jit(solution)/shard_map/ppermute | solution.py:17
  85.1 1.3 collective-permute-done.9
  88.0 4.6 %collective-permute-start.11 = (f32[4,10,10,1]{3,1,2,0:T(8,128)S(1)}, f32[4,10,10,1]{3,1,2,0:T(8,128)S(1)}, u32[]{:S(2)}, u32[]{:S(2)}) collective-permute-start(f32[4,10,10,1]{3,1,2,0:T(8,128)S(1)} %get-tuple-element.28), channel_id=1, source_target_pairs={{0,1},{2,3},{4,5},{6,7},{8,9},{10,11},{12,13},{14,15},{16,17},{18,... | collective-permute-start | bytes 4808 | tf_op jit(solution)/shard_map/ppermute | solution.py:17
  92.8 5.2 %collective-permute-done.10 = f32[4,10,10,1]{3,1,2,0:T(8,128)S(1)} collective-permute-done((f32[4,10,10,1]{3,1,2,0:T(8,128)S(1)}, f32[4,10,10,1]{3,1,2,0:T(8,128)S(1)}, u32[]{:S(2)}, u32[]{:S(2)}) %collective-permute-start.10) | collective-permute-done | bytes 1632 | tf_op jit(solution)/shard_map/ppermute | solution.py:20
  99.7 41.8 %all-reduce.1 = (f32[4]{0:T(128)S(1)}, f32[4]{0:T(128)S(1)}) all-reduce(f32[4]{0:T(128)S(1)} %get-tuple-element.7, f32[4]{0:T(128)S(1)} %get-tuple-element.6), channel_id=1, replica_groups=mesh['gx'=4,'gy'=4,'gz'=2] {'gx','gy','gz'}, use_global_device_ids=true, to_apply=%region_2.3 | all-reduce | flops 8 | bytes 64 | tf_op jit(solution)/shard_map/psum | solution.py:117
  141.7 1.3 collective-permute-start.12
  143.0 3.0 %collective-permute-start.13 = (f32[4,1,8,128]{3,1,2,0:T(1,128)S(1)}, f32[4,1,8,128]{3,1,2,0:T(1,128)S(1)}, u32[]{:S(2)}, u32[]{:S(2)}) collective-permute-start(f32[4,1,8,128]{3,1,2,0:T(1,128)S(1)} %get-tuple-element.37), channel_id=1, source_target_pairs={{0,8},{8,16},{16,24},{1,9},{9,17},{17,25},{2,10},{10,18},{18,26},{... | collective-permute-start | bytes 49160 | tf_op jit(solution)/shard_map/ppermute | solution.py:17
  148.2 4.5 %collective-permute-start.15 = (f32[4,10,1,128]{3,1,2,0:T(8,128)S(1)}, f32[4,10,1,128]{3,1,2,0:T(8,128)S(1)}, u32[]{:S(2)}, u32[]{:S(2)}) collective-permute-start(f32[4,10,1,128]{3,1,2,0:T(8,128)S(1)} %get-tuple-element.31), channel_id=1, source_target_pairs={{0,2},{2,4},{4,6},{1,3},{3,5},{5,7},{8,10},{10,12},{12,14},{9,11},... | collective-permute-start | bytes 61448 | tf_op jit(solution)/shard_map/ppermute | solution.py:17
  153.0 1.3 collective-permute-done.15
  155.9 4.6 %collective-permute-start.17 = (f32[4,10,10,1]{3,1,2,0:T(8,128)S(1)}, f32[4,10,10,1]{3,1,2,0:T(8,128)S(1)}, u32[]{:S(2)}, u32[]{:S(2)}) collective-permute-start(f32[4,10,10,1]{3,1,2,0:T(8,128)S(1)} %get-tuple-element.26), channel_id=1, source_target_pairs={{0,1},{2,3},{4,5},{6,7},{8,9},{10,11},{12,13},{14,15},{16,17},{18,... | collective-permute-start | bytes 4808 | tf_op jit(solution)/shard_map/ppermute | solution.py:17
  160.7 6.1 %collective-permute-done.16 = f32[4,10,10,1]{3,1,2,0:T(8,128)S(1)} collective-permute-done((f32[4,10,10,1]{3,1,2,0:T(8,128)S(1)}, f32[4,10,10,1]{3,1,2,0:T(8,128)S(1)}, u32[]{:S(2)}, u32[]{:S(2)}) %collective-permute-start.16) | collective-permute-done | bytes 1632 | tf_op jit(solution)/shard_map/ppermute | solution.py:20
  168.5 41.7 %all-reduce = (f32[4]{0:T(128)S(1)}, f32[4]{0:T(128)S(1)}, f32[4,8,8]{2,1,0:T(8,128)S(1)}) all-reduce(f32[4]{0:T(128)S(1)} %get-tuple-element.23, f32[4]{0:T(128)S(1)} %fusion.11, f32[4,8,8]{2,1,0:T(8,128)S(1)} %convolution_bitcast_fusion.3), channel_id=1, replica_groups=mesh['gx'=4,'gy'=4,'gz'=2] {'gx','gy','gz'}, use_global_device_ids=true, to_apply=%region_6.7 | all-reduce | flops 264 | bytes 2112 | tf_op jit(solution)/shard_map/psum | solution.py:119
  211.2 1.6 fusion.16
  212.8 21.1 %all-reduce.2 = (f32[4,8]{1,0:T(4,128)S(1)}, f32[4]{0:T(128)S(1)}) all-reduce(f32[4,8]{1,0:T(4,128)S(1)} %bitcast.129, f32[4]{0:T(128)S(1)} %get-tuple-element.19), channel_id=1, replica_groups=mesh['gx'=4,'gy'=4,'gz'=2] {'gy','gz'}, use_global_device_ids=true, to_apply=%region_9.10 | all-reduce | flops 36 | bytes 288 | tf_op jit(solution)/shard_map/psum | solution.py:134
  233.9 5.6 %all-reduce.3 = (f32[4,8]{1,0:T(4,128)S(1)}, f32[4]{0:T(128)S(1)}) all-reduce(f32[4,8]{1,0:T(4,128)S(1)} %get-tuple-element.15, f32[4]{0:T(128)S(1)} %get-tuple-element.16), channel_id=1, replica_groups=mesh['gx'=4,'gy'=4,'gz'=2] {'gx'}, use_global_device_ids=true, to_apply=%region_10.11 | all-reduce | flops 36 | bytes 288 | tf_op jit(solution)/shard_map/psum | solution.py:133
  (75 shorter events, 22.9 us)
Async XLA Ops:
  0.6 49.8 %copy-start = (f32[8,8]{1,0:T(8,128)S(1)}, f32[8,8]{1,0:T(8,128)}, u32[]{:S(2)}) copy-start(f32[8,8]{1,0:T(8,128)} %param.9) | copy-start | bytes 772
  0.6 44.6 %copy-start.1 = (bf16[4,8,8,8,128]{4,3,2,1,0:T(8,128)(2,1)S(1)}, bf16[4,8,8,8,128]{4,3,2,1,0:T(8,128)(2,1)}, u32[]{:S(2)}) copy-start(bf16[4,8,8,8,128]{4,3,2,1,0:T(8,128)(2,1)} %param.6) | copy-start | bytes 1572868
  46.0 5.6 %collective-permute-start = (f32[4,1,8,128]{3,1,2,0:T(1,128)S(1)}, f32[4,1,8,128]{3,1,2,0:T(1,128)S(1)}, u32[]{:S(2)}, u32[]{:S(2)}) collective-permute-start(f32[4,1,8,128]{3,1,2,0:T(1,128)S(1)} %get-tuple-element.42), channel_id=1, source_target_pairs={{8,0},{16,8},{24,16},{9,1},{17,9},{25,17},{10,2},{18,10},{26,18},{... | collective-permute-start | bytes 49160 | tf_op jit(solution)/shard_map/ppermute | solution.py:20
  47.3 4.3 %collective-permute-start.1 = (f32[4,1,8,128]{3,1,2,0:T(1,128)S(1)}, f32[4,1,8,128]{3,1,2,0:T(1,128)S(1)}, u32[]{:S(2)}, u32[]{:S(2)}) collective-permute-start(f32[4,1,8,128]{3,1,2,0:T(1,128)S(1)} %get-tuple-element.41), channel_id=1, source_target_pairs={{0,8},{8,16},{16,24},{1,9},{9,17},{17,25},{2,10},{10,18},{18,26},{... | collective-permute-start | bytes 49160 | tf_op jit(solution)/shard_map/ppermute | solution.py:17
  51.6 5.9 %collective-permute-start.2 = (f32[4,10,1,128]{3,1,2,0:T(8,128)S(1)}, f32[4,10,1,128]{3,1,2,0:T(8,128)S(1)}, u32[]{:S(2)}, u32[]{:S(2)}) collective-permute-start(f32[4,10,1,128]{3,1,2,0:T(8,128)S(1)} %get-tuple-element.36), channel_id=1, source_target_pairs={{2,0},{4,2},{6,4},{3,1},{5,3},{7,5},{10,8},{12,10},{14,12},{11,9},... | collective-permute-start | bytes 61448 | tf_op jit(solution)/shard_map/ppermute | solution.py:20
  52.9 6.1 %collective-permute-start.3 = (f32[4,10,1,128]{3,1,2,0:T(8,128)S(1)}, f32[4,10,1,128]{3,1,2,0:T(8,128)S(1)}, u32[]{:S(2)}, u32[]{:S(2)}) collective-permute-start(f32[4,10,1,128]{3,1,2,0:T(8,128)S(1)} %get-tuple-element.35), channel_id=1, source_target_pairs={{0,2},{2,4},{4,6},{1,3},{3,5},{5,7},{8,10},{10,12},{12,14},{9,11},... | collective-permute-start | bytes 61448 | tf_op jit(solution)/shard_map/ppermute | solution.py:17
  59.1 6.1 %copy-start.2 = (f32[8,8,128]{2,1,0:T(8,128)S(1)}, f32[8,8,128]{2,1,0:T(8,128)}, u32[]{:S(2)}) copy-start(f32[8,8,128]{2,1,0:T(8,128)} %param.7) | copy-start | bytes 98308
  59.1 13.6 %copy-start.3 = (f32[4,8,8,128]{3,2,1,0:T(8,128)S(1)}, f32[4,8,8,128]{3,2,1,0:T(8,128)}, u32[]{:S(2)}) copy-start(f32[4,8,8,128]{3,2,1,0:T(8,128)} %param.5) | copy-start | bytes 393220
  59.3 12.3 %collective-permute-start.4 = (f32[4,10,10,1]{3,1,2,0:T(8,128)S(1)}, f32[4,10,10,1]{3,1,2,0:T(8,128)S(1)}, u32[]{:S(2)}, u32[]{:S(2)}) collective-permute-start(f32[4,10,10,1]{3,1,2,0:T(8,128)S(1)} %get-tuple-element.29), channel_id=1, source_target_pairs={{1,0},{3,2},{5,4},{7,6},{9,8},{11,10},{13,12},{15,14},{17,16},{19,... | collective-permute-start | bytes 4808 | tf_op jit(solution)/shard_map/ppermute | solution.py:20
  60.6 12.2 %collective-permute-start.5 = (f32[4,10,10,1]{3,1,2,0:T(8,128)S(1)}, f32[4,10,10,1]{3,1,2,0:T(8,128)S(1)}, u32[]{:S(2)}, u32[]{:S(2)}) collective-permute-start(f32[4,10,10,1]{3,1,2,0:T(8,128)S(1)} %get-tuple-element.30), channel_id=1, source_target_pairs={{0,1},{2,3},{4,5},{6,7},{8,9},{10,11},{12,13},{14,15},{16,17},{18,... | collective-permute-start | bytes 4808 | tf_op jit(solution)/shard_map/ppermute | solution.py:17
  72.7 0.7 copy-start.4
  73.8 4.3 %collective-permute-start.6 = (f32[4,1,8,128]{3,1,2,0:T(1,128)S(1)}, f32[4,1,8,128]{3,1,2,0:T(1,128)S(1)}, u32[]{:S(2)}, u32[]{:S(2)}) collective-permute-start(f32[4,1,8,128]{3,1,2,0:T(1,128)S(1)} %get-tuple-element.40), channel_id=1, source_target_pairs={{8,0},{16,8},{24,16},{9,1},{17,9},{25,17},{10,2},{18,10},{26,18},{... | collective-permute-start | bytes 49160 | tf_op jit(solution)/shard_map/ppermute | solution.py:20
  75.1 3.9 %collective-permute-start.7 = (f32[4,1,8,128]{3,1,2,0:T(1,128)S(1)}, f32[4,1,8,128]{3,1,2,0:T(1,128)S(1)}, u32[]{:S(2)}, u32[]{:S(2)}) collective-permute-start(f32[4,1,8,128]{3,1,2,0:T(1,128)S(1)} %get-tuple-element.39), channel_id=1, source_target_pairs={{0,8},{8,16},{16,24},{1,9},{9,17},{17,25},{2,10},{10,18},{18,26},{... | collective-permute-start | bytes 49160 | tf_op jit(solution)/shard_map/ppermute | solution.py:17
  79.0 6.1 %collective-permute-start.8 = (f32[4,10,1,128]{3,1,2,0:T(8,128)S(1)}, f32[4,10,1,128]{3,1,2,0:T(8,128)S(1)}, u32[]{:S(2)}, u32[]{:S(2)}) collective-permute-start(f32[4,10,1,128]{3,1,2,0:T(8,128)S(1)} %get-tuple-element.34), channel_id=1, source_target_pairs={{2,0},{4,2},{6,4},{3,1},{5,3},{7,5},{10,8},{12,10},{14,12},{11,9},... | collective-permute-start | bytes 61448 | tf_op jit(solution)/shard_map/ppermute | solution.py:20
  80.3 6.1 %collective-permute-start.9 = (f32[4,10,1,128]{3,1,2,0:T(8,128)S(1)}, f32[4,10,1,128]{3,1,2,0:T(8,128)S(1)}, u32[]{:S(2)}, u32[]{:S(2)}) collective-permute-start(f32[4,10,1,128]{3,1,2,0:T(8,128)S(1)} %get-tuple-element.33), channel_id=1, source_target_pairs={{0,2},{2,4},{4,6},{1,3},{3,5},{5,7},{8,10},{10,12},{12,14},{9,11},... | collective-permute-start | bytes 61448 | tf_op jit(solution)/shard_map/ppermute | solution.py:17
  86.7 11.4 %collective-permute-start.10 = (f32[4,10,10,1]{3,1,2,0:T(8,128)S(1)}, f32[4,10,10,1]{3,1,2,0:T(8,128)S(1)}, u32[]{:S(2)}, u32[]{:S(2)}) collective-permute-start(f32[4,10,10,1]{3,1,2,0:T(8,128)S(1)} %get-tuple-element.27), channel_id=1, source_target_pairs={{1,0},{3,2},{5,4},{7,6},{9,8},{11,10},{13,12},{15,14},{17,16},{19,... | collective-permute-start | bytes 4808 | tf_op jit(solution)/shard_map/ppermute | solution.py:20
  88.0 11.3 %collective-permute-start.11 = (f32[4,10,10,1]{3,1,2,0:T(8,128)S(1)}, f32[4,10,10,1]{3,1,2,0:T(8,128)S(1)}, u32[]{:S(2)}, u32[]{:S(2)}) collective-permute-start(f32[4,10,10,1]{3,1,2,0:T(8,128)S(1)} %get-tuple-element.28), channel_id=1, source_target_pairs={{0,1},{2,3},{4,5},{6,7},{8,9},{10,11},{12,13},{14,15},{16,17},{18,... | collective-permute-start | bytes 4808 | tf_op jit(solution)/shard_map/ppermute | solution.py:17
  141.7 4.9 %collective-permute-start.12 = (f32[4,1,8,128]{3,1,2,0:T(1,128)S(1)}, f32[4,1,8,128]{3,1,2,0:T(1,128)S(1)}, u32[]{:S(2)}, u32[]{:S(2)}) collective-permute-start(f32[4,1,8,128]{3,1,2,0:T(1,128)S(1)} %get-tuple-element.38), channel_id=1, source_target_pairs={{8,0},{16,8},{24,16},{9,1},{17,9},{25,17},{10,2},{18,10},{26,18},{... | collective-permute-start | bytes 49160 | tf_op jit(solution)/shard_map/ppermute | solution.py:20
  143.0 3.9 %collective-permute-start.13 = (f32[4,1,8,128]{3,1,2,0:T(1,128)S(1)}, f32[4,1,8,128]{3,1,2,0:T(1,128)S(1)}, u32[]{:S(2)}, u32[]{:S(2)}) collective-permute-start(f32[4,1,8,128]{3,1,2,0:T(1,128)S(1)} %get-tuple-element.37), channel_id=1, source_target_pairs={{0,8},{8,16},{16,24},{1,9},{9,17},{17,25},{2,10},{10,18},{18,26},{... | collective-permute-start | bytes 49160 | tf_op jit(solution)/shard_map/ppermute | solution.py:17
  146.9 6.1 %collective-permute-start.14 = (f32[4,10,1,128]{3,1,2,0:T(8,128)S(1)}, f32[4,10,1,128]{3,1,2,0:T(8,128)S(1)}, u32[]{:S(2)}, u32[]{:S(2)}) collective-permute-start(f32[4,10,1,128]{3,1,2,0:T(8,128)S(1)} %get-tuple-element.32), channel_id=1, source_target_pairs={{2,0},{4,2},{6,4},{3,1},{5,3},{7,5},{10,8},{12,10},{14,12},{11,9},... | collective-permute-start | bytes 61448 | tf_op jit(solution)/shard_map/ppermute | solution.py:20
  148.2 6.1 %collective-permute-start.15 = (f32[4,10,1,128]{3,1,2,0:T(8,128)S(1)}, f32[4,10,1,128]{3,1,2,0:T(8,128)S(1)}, u32[]{:S(2)}, u32[]{:S(2)}) collective-permute-start(f32[4,10,1,128]{3,1,2,0:T(8,128)S(1)} %get-tuple-element.31), channel_id=1, source_target_pairs={{0,2},{2,4},{4,6},{1,3},{3,5},{5,7},{8,10},{10,12},{12,14},{9,11},... | collective-permute-start | bytes 61448 | tf_op jit(solution)/shard_map/ppermute | solution.py:17
  154.6 12.3 %collective-permute-start.16 = (f32[4,10,10,1]{3,1,2,0:T(8,128)S(1)}, f32[4,10,10,1]{3,1,2,0:T(8,128)S(1)}, u32[]{:S(2)}, u32[]{:S(2)}) collective-permute-start(f32[4,10,10,1]{3,1,2,0:T(8,128)S(1)} %get-tuple-element.25), channel_id=1, source_target_pairs={{1,0},{3,2},{5,4},{7,6},{9,8},{11,10},{13,12},{15,14},{17,16},{19,... | collective-permute-start | bytes 4808 | tf_op jit(solution)/shard_map/ppermute | solution.py:20
  155.9 12.2 %collective-permute-start.17 = (f32[4,10,10,1]{3,1,2,0:T(8,128)S(1)}, f32[4,10,10,1]{3,1,2,0:T(8,128)S(1)}, u32[]{:S(2)}, u32[]{:S(2)}) collective-permute-start(f32[4,10,10,1]{3,1,2,0:T(8,128)S(1)} %get-tuple-element.26), channel_id=1, source_target_pairs={{0,1},{2,3},{4,5},{6,7},{8,9},{10,11},{12,13},{14,15},{16,17},{18,... | collective-permute-start | bytes 4808 | tf_op jit(solution)/shard_map/ppermute | solution.py:17
